TPU v7x, 32 devices: a whole 2x2x4 slice. The times are simulated.
32 devices in a mesh: seq: 32 (over z, y, x, core).
Axes of the slice: x: 2, y: 2, z: 4, core: 2. Of those that a mesh axis runs over, the one named last changes fastest.
Arguments:
- queries: bfloat16 [16, 8192], P(None, 'seq'), may hold values from -1000 to 1000
- span_keys: bfloat16 [16, 1024], P(None, 'seq'), may hold values from -6 to 6
- span_values: bfloat16 [16, 1024], P(None, 'seq'), may hold values from -6 to 6
- positions: int32 [3, 16], replicated, may hold values from 0 to 8191, as said below
- span_segments: int32 [16], replicated, may hold values from 0 to 3, as said below
- cache_keys: bfloat16 [16384, 1024], P('seq'), may hold values from -6 to 6
- cache_values: bfloat16 [16384, 1024], P('seq'), may hold values from -6 to 6
- cache_segments: int32 [16384], P('seq'), may hold values from 0 to 3
Outputs:
- attended: bfloat16 [16, 8192], replicated
Inputs may be any that keep to these rules, and one draw needn't show every extreme that they name: `positions`: row 0 holds time ids; rows 1 and 2 hold height and width ids, which are below 64. `span_segments`: never falling; every request 0 to 3 has one run of rows, and every run starts at an even row.
All inputs are finite; a program needn't handle non-finite values.
Results may differ from a plain program's by a relative error of at most 0.0054.
Values may be sent and summed in bfloat16 or wider, within the bound.
A program may use at most 64 MiB of HBM per device.

v0:
```python
import jax
import jax.numpy as jnp
from jax import lax
from jax.sharding import PartitionSpec as P

H = 64
KVH = 8
HD = 128


def rope_tables(positions, head_dim):
    half = head_dim // 2
    index = jnp.arange(half, dtype=jnp.int32)
    inverse = jnp.power(jnp.float32(1000000.0), -2.0 * index.astype(jnp.float32) / head_dim)
    section = jnp.where(index < head_dim // 8, 0, jnp.where(index < 5 * head_dim // 16, 1, 2))
    chosen = jnp.where(
        section[None, :] == 0,
        positions[0][:, None],
        jnp.where(section[None, :] == 1, positions[1][:, None], positions[2][:, None]),
    )
    angle = chosen.astype(jnp.float32) * inverse[None, :]
    return (jnp.cos(angle), jnp.sin(angle))


def rotate(values, cosines, sines):
    half = values.shape[-1] // 2
    first = values[..., :half]
    second = values[..., half:]
    cosine = cosines[:, None, :]
    sine = sines[:, None, :]
    return jnp.concatenate(
        [first * cosine - second * sine, second * cosine + first * sine], axis=-1
    )


def head_state(q_rot, keys, values, visible):
    rows, kv_heads, group, head_dim = q_rot.shape
    scale = 1.0 / head_dim**0.5
    outs, peaks, totals = ([], [], [])
    for head in range(kv_heads):
        block = q_rot[:, head].reshape(rows * group, head_dim)
        key_cols = keys[:, head * head_dim : (head + 1) * head_dim]
        value_cols = values[:, head * head_dim : (head + 1) * head_dim]
        scores = (
            lax.dot_general(
                block, key_cols, (((1,), (1,)), ((), ())), preferred_element_type=jnp.float32
            )
            * scale
        )
        scores = scores.reshape(rows, group, -1)
        mask = visible[:, None, :]
        peak = jnp.max(jnp.where(mask, scores, jnp.float32(-1e30)), axis=-1)
        weights = jnp.where(mask, jnp.exp(scores - peak[..., None]), jnp.float32(0.0))
        total = jnp.sum(weights, axis=-1)
        out = jnp.dot(
            weights.astype(jnp.bfloat16).reshape(rows * group, -1),
            value_cols,
            preferred_element_type=jnp.float32,
        )
        outs.append(out.reshape(rows, group, head_dim))
        peaks.append(peak)
        totals.append(total)
    out_all = jnp.stack(outs, axis=1).reshape(rows * kv_heads * group, head_dim)
    peak_all = jnp.stack(peaks, axis=1).reshape(rows * kv_heads * group)
    total_all = jnp.stack(totals, axis=1).reshape(rows * kv_heads * group)
    return (out_all, peak_all, total_all)


def combine(left, right):
    out_a, peak_a, total_a = left
    out_b, peak_b, total_b = right
    peak = jnp.maximum(peak_a, peak_b)
    factor_a = jnp.exp(peak_a - peak)
    factor_b = jnp.exp(peak_b - peak)
    return (
        out_a * factor_a[:, None] + out_b * factor_b[:, None],
        peak,
        total_a * factor_a + total_b * factor_b,
    )


def per_device(
    queries,
    span_keys,
    span_values,
    positions,
    span_segments,
    cache_keys,
    cache_values,
    cache_segments,
):
    whole_queries, whole_keys, whole_values = (
        lax.all_gather(queries, "seq", axis=1, tiled=True),
        lax.all_gather(span_keys, "seq", axis=1, tiled=True),
        lax.all_gather(span_values, "seq", axis=1, tiled=True),
    )
    rows = whole_queries.shape[0]
    group = H // KVH
    cosines, sines = rope_tables(positions, HD)
    q_rot = rotate(whole_queries.astype(jnp.float32).reshape(rows, H, HD), cosines, sines).astype(
        jnp.bfloat16
    )
    q_rot = q_rot.reshape(rows, KVH, group, HD)
    k_rot = rotate(whole_keys.astype(jnp.float32).reshape(rows, KVH, HD), cosines, sines)
    k_rot = k_rot.astype(jnp.bfloat16).reshape(rows, KVH * HD)
    index = jnp.arange(rows, dtype=jnp.int32)
    own_visible = (span_segments[:, None] == span_segments[None, :]) & (
        index[None, :] <= index[:, None]
    )
    span_state = head_state(q_rot, k_rot, whole_values, own_visible)
    visible = span_segments[:, None] == cache_segments[None, :]
    local_state = head_state(q_rot, cache_keys, cache_values, visible)
    local_out, local_peak, local_total = local_state
    peak = lax.pmax(local_peak, "seq")
    factor = jnp.exp(local_peak - peak)
    shares, totals = (
        lax.psum_scatter(local_out * factor[:, None], "seq", scatter_dimension=0, tiled=True),
        lax.psum_scatter(local_total * factor, "seq", scatter_dimension=0, tiled=True),
    )
    count = totals.shape[0]
    start = lax.axis_index("seq") * count
    own_out = lax.dynamic_slice_in_dim(span_state[0], start, count, 0)
    own_peak = lax.dynamic_slice_in_dim(span_state[1], start, count, 0)
    own_total = lax.dynamic_slice_in_dim(span_state[2], start, count, 0)
    mine_peak = lax.dynamic_slice_in_dim(peak, start, count, 0)
    merged_out, _, merged_total = combine(
        (shares, mine_peak, totals), (own_out, own_peak, own_total)
    )
    finished = (merged_out / merged_total[:, None]).astype(jnp.bfloat16)
    gathered = lax.all_gather(finished, "seq", axis=0, tiled=True)
    return gathered.reshape(rows, H * HD)


def solution(mesh):
    in_specs = (
        P(None, "seq"),
        P(None, "seq"),
        P(None, "seq"),
        P(),
        P(),
        P("seq", None),
        P("seq", None),
        P("seq"),
    )
    out_specs = P()
    return jax.shard_map(
        per_device, mesh=mesh, in_specs=in_specs, out_specs=out_specs, check_vma=False
    )
```

profile of v0, /device:TPU:0, one launch (start us, length us, event | category | flops | bytes accessed | tf_op | source)
XLA Modules:
  0.0 285.4 jit_solution(309847367351104898)
XLA Ops:
  6.6 0.7 copy-done.29
  7.2 44.2 %all_gather.12 = bf16[16,8192]{1,0:T(8,128)(2,1)S(1)} all-gather(bf16[16,256]{1,0:T(8,128)(2,1)} %param.8), channel_id=1, replica_groups=mesh['seq'=32] {'seq'}, dimensions={1}, use_global_device_ids=true | all-gather | bytes 270336 | tf_op jit(solution)/shard_map/all_gather | solution.py:93
  51.7 0.2 fusion.17
  52.0 0.3 copy-done.2
  52.4 0.5 copy-done.1
  54.2 0.4 copy-done.23
  54.7 0.3 fusion.25
  55.2 0.4 copy-done.19
  55.5 0.9 fusion.40
  57.2 36.9 %pmax.7 = f32[1024]{0:T(1024)} all-reduce(f32[1024]{0:T(1024)S(1)} %reshape.621), channel_id=1, replica_groups=mesh['seq'=32] {'seq'}, use_global_device_ids=true, to_apply=%region_8.9 | all-reduce | flops 1024 | bytes 8192 | tf_op jit(solution)/shard_map/pmax | solution.py:114
  94.1 0.5 fusion.38
  95.3 0.7 copy-done.28
  96.3 0.5 copy-done.22
  97.0 0.4 copy-done.18
  97.7 0.4 copy-done.16
  98.1 0.2 fusion.13
  98.3 0.4 copy-done.14
  98.9 0.4 copy-done.12
  99.5 0.4 copy-done.10
  100.1 0.4 copy-done.8
  100.8 0.4 copy-done.20
  101.5 0.6 copy-done.5
  102.1 1.0 bitcast_multiply_fusion
  103.2 0.7 copy-done.25
  103.8 40.8 %all-gather = bf16[32,32,16]{1,2,0:T(8,128)(2,1)S(1)} all-gather(bf16[1,32,16]{1,2,0:T(8,128)(2,1)S(1)} %bitcast.347), channel_id=1, replica_groups=mesh['seq'=32] {'seq'}, dimensions={0}, use_global_device_ids=true | all-gather | bytes 33792 | tf_op jit(solution)/shard_map/all_gather | solution.py:94
  144.8 0.7 copy-done.3
  148.7 37.0 %all-gather.1 = bf16[32,32,16]{1,2,0:T(8,128)(2,1)S(1)} all-gather(bf16[1,32,16]{1,2,0:T(8,128)(2,1)S(1)} %bitcast.348), channel_id=1, replica_groups=mesh['seq'=32] {'seq'}, dimensions={0}, use_global_device_ids=true | all-gather | bytes 33792 | tf_op jit(solution)/shard_map/all_gather | solution.py:95
  188.3 36.9 %all-reduce = f32[1024]{0:T(1024)S(1)} all-reduce(f32[1024]{0:T(1024)S(1)} %get-tuple-element.40), channel_id=3, replica_groups=mesh['seq'=32] {'seq'}, use_global_device_ids=true, to_apply=%region_26.27.clone | all-reduce | flops 1024 | bytes 8192
  225.3 14.6 %reduce-scatter.2.cloned.1.call-done = f32[32,128]{1,0:T(8,128)} async-done(((f32[1024,128]{1,0:T(8,128)}), f32[32,128]{1,0:T(8,128)}) %reduce-scatter.2.cloned.1.call-update) | async-done | bytes 16400 | tf_op jit(solution)/shard_map/reduce_scatter | solution.py:117
  239.9 0.8 divide_convert_fusion
  240.7 37.0 %all_gather.15 = bf16[1024,128]{1,0:T(8,128)(2,1)S(1)} all-gather(bf16[32,128]{1,0:T(8,128)(2,1)S(1)} %divide_convert_fusion), channel_id=1, replica_groups=mesh['seq'=32] {'seq'}, dimensions={0}, use_global_device_ids=true | all-gather | bytes 270336 | tf_op jit(solution)/shard_map/all_gather | solution.py:130
  277.8 0.8 reshape.636
  (178 shorter events, 11.0 us)
Async XLA Ops:
  6.5 0.7 copy-start.29
  6.5 233.4 %reduce-scatter.2.cloned.1.call-start = ((), (), s32[]{:S(2)}) async-start(), calls=%async_computation.1 | async-start | bytes 540672 | tf_op jit(solution)/shard_map/reduce_scatter | solution.py:117
  51.7 0.6 copy-start.2
  51.7 1.2 copy-start.1
  53.9 0.7 copy-start.23
  53.9 0.7 copy-start.27
  55.0 0.5 copy-start.19
  55.0 0.5 copy-start.21
  56.4 37.6 %copy-start.7 = (f32[128]{0:T(128)}, f32[128]{0:T(128)S(1)}, u32[]{:S(2)}) copy-start(f32[128]{0:T(128)S(1)} %get-tuple-element.6) | copy-start | bytes 1540
  56.5 37.6 %copy-start.9 = (f32[128]{0:T(128)}, f32[128]{0:T(128)S(1)}, u32[]{:S(2)}) copy-start(f32[128]{0:T(128)S(1)} %get-tuple-element.7) | copy-start | bytes 1540
  56.5 37.6 %copy-start.11 = (f32[128]{0:T(128)}, f32[128]{0:T(128)S(1)}, u32[]{:S(2)}) copy-start(f32[128]{0:T(128)S(1)} %get-tuple-element.8) | copy-start | bytes 1540
  56.5 37.6 %copy-start.13 = (f32[128]{0:T(128)}, f32[128]{0:T(128)S(1)}, u32[]{:S(2)}) copy-start(f32[128]{0:T(128)S(1)} %get-tuple-element.9) | copy-start | bytes 1540
  56.5 37.6 %copy-start.15 = (f32[128]{0:T(128)}, f32[128]{0:T(128)S(1)}, u32[]{:S(2)}) copy-start(f32[128]{0:T(128)S(1)} %get-tuple-element.10) | copy-start | bytes 1540
  56.5 37.7 %copy-start.17 = (f32[128]{0:T(128)}, f32[128]{0:T(128)S(1)}, u32[]{:S(2)}) copy-start(f32[128]{0:T(128)S(1)} %get-tuple-element.11) | copy-start | bytes 1540
  57.1 39.1 %copy-start = (bf16[512,1024]{1,0:T(8,128)(2,1)S(1)}, bf16[512,1024]{1,0:T(8,128)(2,1)}, u32[]{:S(2)}) copy-start(bf16[512,1024]{1,0:T(8,128)(2,1)} %param.14) | copy-start | bytes 3145732
  57.2 36.9 %copy-start.4 = (f32[1024]{0:T(1024)}, f32[1024]{0:T(1024)S(1)}, u32[]{:S(2)}) copy-start(f32[1024]{0:T(1024)S(1)} %reshape.621) | copy-start | bytes 12292
  95.3 0.7 copy-start.28
  96.1 0.6 copy-start.22
  96.8 0.7 copy-start.18
  97.4 0.7 copy-start.16
  98.1 0.6 copy-start.14
  98.7 0.6 copy-start.12
  99.3 0.6 copy-start.10
  99.9 0.7 copy-start.8
  100.6 0.6 copy-start.20
  101.4 0.7 copy-start.5
  101.4 0.7 copy-start.6
  103.1 0.7 copy-start.25
  144.8 0.7 copy-start.3
  145.9 0.8 copy-start.24
  147.8 0.9 copy-start.26
Sparse Core Ops, SparseCore 0:
  103.3 136.5 reduce-scatter.1
where the time goes:
time: 286 us; the launch traced here: 285 us
  blocking collectives  233 us (81%)
  waiting for transfers between devices  14.7 us (5%)
  local copies, waits for them, and re-layouts  14.1 us (5%)
  between operations  14.1 us (5%)
  matrix products  6.45 us (2%)
  other arithmetic  3.34 us (1%)
    all_gather x1, blocking collectives, per_device(): lax.all_gather(queries, 'seq', axis=1, tiled=True)  44.2 us
    all_gather x1, blocking collectives, per_device(): lax.all_gather(span_keys, 'seq', axis=1, tiled=True)  40.8 us
    all_gather x1, blocking collectives, per_device(): gathered = lax.all_gather(finished, 'seq', axis=0, tiled=True)  37 us
    all_gather x1, blocking collectives, per_device(): lax.all_gather(span_values, 'seq', axis=1, tiled=True)  37 us
    unnamed x1, blocking collectives  36.9 us
    pmax x1, blocking collectives, per_device(): peak = lax.pmax(local_peak, 'seq')  36.9 us
    reduce_scatter x1, waiting for transfers between devices, per_device(): lax.psum_scatter(local_out * factor[:, None], 'seq', scatter_dimension=0,...  14.6 us
    unnamed x92, local copies, waits for them, and re-layouts  8.67 us
  transfers between devices with their start and end apart: 1, of which 1 were waited for; matrix products, arithmetic and copies ran while one was open for 2% of the time, Pallas kernels for 0%

commit v1 on v0

v1 whole, which is shorter than its diff:
```python
import functools
import math

import jax
import jax.numpy as jnp
import numpy as np
from jax import lax
from jax.experimental import pallas as pl
from jax.experimental.pallas import tpu as pltpu
from jax.sharding import PartitionSpec as P

H = 64
KVH = 8
HD = 128
MESH = pl.DeviceIdType.MESH
HIDDEN = -1e30
FLOOR = -1e29


def rope_tables(pos, rows):
    half = HD // 2
    lane = lax.broadcasted_iota(jnp.int32, (rows, HD), 1)
    row = lax.broadcasted_iota(jnp.int32, (rows, HD), 0)
    index = lax.rem(lane, half)
    inverse = jnp.zeros((rows, HD), jnp.float32)
    for j in range(half):
        inverse = jnp.where(index == j, jnp.float32(np.float32(1e6 ** (-2.0 * j / HD))), inverse)
    chosen = []
    for c in range(3):
        spread = jnp.zeros((rows, HD), jnp.int32)
        for r in range(rows):
            spread = jnp.where(row == r, pos[c, r], spread)
        chosen.append(spread)
    picked = jnp.where(
        index < HD // 8, chosen[0], jnp.where(index < 5 * HD // 16, chosen[1], chosen[2])
    )
    angle = picked.astype(jnp.float32) * inverse
    sine = jnp.sin(angle)
    return jnp.cos(angle), jnp.where(lane < half, -sine, sine)


def columns(buf, start, width):
    if width >= HD:
        slot, off = start // width, start % width
        return buf[slot, :, off : off + HD].astype(jnp.float32)
    first = start // width
    return jnp.concatenate(
        [buf[first + i].astype(jnp.float32) for i in range(HD // width)], axis=1
    )


def kernel(
    n,
    q_hbm,
    k_hbm,
    v_hbm,
    pos_hbm,
    seg_hbm,
    ck_hbm,
    cv_hbm,
    cs_hbm,
    out_ref,
    q_own,
    k_own,
    v_own,
    pos,
    seg,
    keys,
    values,
    cseg,
    q_all,
    k_all,
    v_all,
    k_span,
    v_span,
    values_t,
    bias,
    part_out,
    part_ml,
    got_out,
    got_ml,
    piece,
    pieces,
    load_sem,
    q_sem,
    kv_sem,
    part_sem,
    ml_sem,
    piece_sem,
    send_sem,
):
    me = lax.axis_index("seq")
    rows, width = q_own.shape
    kwidth = k_own.shape[1]
    tokens = keys.shape[0]
    per = n // KVH
    share = HD // per
    mine = me // per

    loads = [
        pltpu.make_async_copy(src, dst, load_sem.at[i])
        for i, (src, dst) in enumerate(
            (
                (q_hbm, q_own),
                (k_hbm, k_own),
                (v_hbm, v_own),
                (pos_hbm, pos),
                (seg_hbm, seg),
                (cs_hbm, cseg),
                (cv_hbm, values),
                (ck_hbm, keys),
            )
        )
    ]
    for load in loads:
        load.start()

    barrier = pltpu.get_barrier_semaphore()

    @pl.loop(1, n)
    def _(i):
        pl.semaphore_signal(
            barrier, inc=1, device_id=(lax.rem(me + i, n),), device_id_type=MESH
        )

    for load in loads[:3]:
        load.wait()
    own_q = pltpu.make_async_copy(q_own, q_all.at[me], q_sem.at[mine])
    own_q.start()
    pl.semaphore_wait(barrier, n - 1)

    @pl.loop(1, n)
    def _(i):
        pltpu.make_async_remote_copy(
            src_ref=q_own,
            dst_ref=q_all.at[me],
            send_sem=send_sem.at[0],
            recv_sem=q_sem.at[mine],
            device_id=(lax.rem(me + i, n),),
            device_id_type=MESH,
        ).start()

    @pl.when(me != 0)
    def _():
        for i, (src, dst) in enumerate(((k_own, k_all), (v_own, v_all))):
            pltpu.make_async_remote_copy(
                src_ref=src,
                dst_ref=dst.at[me],
                send_sem=send_sem.at[1 + i],
                recv_sem=kv_sem.at[i],
                device_id=(0,),
                device_id_type=MESH,
            ).start()

    @pl.when(me == 0)
    def _():
        for i, (src, dst) in enumerate(((k_own, k_all), (v_own, v_all))):
            pltpu.make_async_copy(src, dst.at[me], kv_sem.at[i]).start()

    for load in loads[3:]:
        load.wait()
    cosine, sine = rope_tables(pos, rows)
    lane = lax.broadcasted_iota(jnp.int32, (1, HD), 1)
    lane_row = lax.rem(lane, rows)
    lane_seg = jnp.zeros((1, HD), jnp.int32)
    for r in range(rows):
        lane_seg = jnp.where(lane_row == r, seg[r], lane_seg)
    lane_seg = lane_seg.astype(jnp.float32)
    for c in range(tokens // HD):
        across = cseg[:, c * HD : (c + 1) * HD].astype(jnp.float32)
        down = jnp.transpose(jnp.broadcast_to(across, (HD, HD)))
        bias[c * HD : (c + 1) * HD, :] = jnp.where(down == lane_seg, 0.0, HIDDEN)
    token = lax.broadcasted_iota(jnp.int32, (rows, HD), 0)
    token_seg = jnp.zeros((rows, HD), jnp.int32)
    for r in range(rows):
        token_seg = jnp.where(token == r, seg[r], token_seg)
    seen = (token_seg.astype(jnp.float32) == lane_seg) & (token <= lane_row)
    holder = jnp.where(me == 0, 0.0, HIDDEN)
    span_bias = jnp.where(seen, holder, HIDDEN)
    for g in range(KVH):
        values_t[g] = jnp.transpose(values[:, g * HD : (g + 1) * HD])

    @pl.when(me == 0)
    def _():
        for i, dst in enumerate((k_all, v_all)):
            pltpu.make_async_copy(dst, dst, kv_sem.at[i]).wait()
        for g in range(KVH):
            cols = slice(g * HD, (g + 1) * HD)
            k = columns(k_all, g * HD, kwidth)
            k_span[:, cols] = (k * cosine + pltpu.roll(k, HD // 2, 1) * sine).astype(jnp.bfloat16)
            v_span[:, cols] = columns(v_all, g * HD, kwidth).astype(jnp.bfloat16)

    @pl.when(me != 0)
    def _():
        k_span[...] = jnp.zeros_like(k_span)
        v_span[...] = jnp.zeros_like(v_span)

    contract_last = (((1,), (1,)), ((), ()))
    contract_first = (((0,), (0,)), ((), ()))
    factor = math.log2(math.e) / math.sqrt(HD)
    group = H // KVH
    for g in range(KVH):
        cols = slice(g * HD, (g + 1) * HD)
        landed = q_all.at[pl.ds(g * per, per)]
        pltpu.make_async_copy(landed, landed, q_sem.at[g]).wait()
        heads = []
        for i in range(group):
            q = columns(q_all, (g * group + i) * HD, width)
            heads.append((q * cosine + pltpu.roll(q, HD // 2, 1) * sine).astype(jnp.bfloat16))
        block = jnp.concatenate(heads, axis=0)
        scores = (
            lax.dot_general(keys[:, cols], block, contract_last, preferred_element_type=jnp.float32)
            + bias[...]
        )
        span_scores = (
            lax.dot_general(
                k_span[:, cols], block, contract_last, preferred_element_type=jnp.float32
            )
            + span_bias
        )
        peak = jnp.maximum(
            jnp.max(scores, axis=0, keepdims=True), jnp.max(span_scores, axis=0, keepdims=True)
        )
        peak = jnp.maximum(peak, FLOOR)
        weights = jnp.exp2((scores - peak) * factor)
        span_weights = jnp.exp2((span_scores - peak) * factor)
        total = jnp.sum(weights, axis=0, keepdims=True) + jnp.sum(
            span_weights, axis=0, keepdims=True
        )
        out = jnp.dot(
            values_t[g], weights.astype(jnp.bfloat16), preferred_element_type=jnp.float32
        ) + lax.dot_general(
            v_span[:, cols],
            span_weights.astype(jnp.bfloat16),
            contract_first,
            preferred_element_type=jnp.float32,
        )
        part_ml[g, 0:1, :] = peak
        part_ml[g, 1:2, :] = total
        for j in range(per):
            part_out[g * per + j] = out[j * share : (j + 1) * share].astype(jnp.bfloat16)

        @pl.loop(0, per)
        def _(j):
            dest = g * per + j

            @pl.when(dest != me)
            def _():
                pltpu.make_async_remote_copy(
                    src_ref=part_out.at[dest],
                    dst_ref=got_out.at[me],
                    send_sem=send_sem.at[3],
                    recv_sem=part_sem,
                    device_id=(dest,),
                    device_id_type=MESH,
                ).start()
                pltpu.make_async_remote_copy(
                    src_ref=part_ml.at[g],
                    dst_ref=got_ml.at[me],
                    send_sem=send_sem.at[4],
                    recv_sem=ml_sem,
                    device_id=(dest,),
                    device_id_type=MESH,
                ).start()

            @pl.when(dest == me)
            def _():
                pltpu.make_async_copy(part_out.at[dest], got_out.at[me], part_sem).start()
                pltpu.make_async_copy(part_ml.at[g], got_ml.at[me], ml_sem).start()

    pltpu.make_async_copy(got_ml, got_ml, ml_sem).wait()
    peaks = got_ml[:, 0, :]
    scale = jnp.exp2((peaks - jnp.max(peaks, axis=0, keepdims=True)) * factor)
    whole = jnp.sum(scale * got_ml[:, 1, :], axis=0, keepdims=True)
    scale = scale / whole
    pltpu.make_async_copy(got_out, got_out, part_sem).wait()
    merged = jnp.zeros((share, HD), jnp.float32)
    for s in range(n):
        merged = merged + got_out[s].astype(jnp.float32) * scale[s : s + 1, :]
    piece[...] = merged.astype(jnp.bfloat16)

    @pl.loop(1, n)
    def _(i):
        pltpu.make_async_remote_copy(
            src_ref=piece,
            dst_ref=pieces.at[me],
            send_sem=send_sem.at[5],
            recv_sem=piece_sem.at[mine],
            device_id=(lax.rem(me + i, n),),
            device_id_type=MESH,
        ).start()

    pltpu.make_async_copy(piece, pieces.at[me], piece_sem.at[mine]).start()

    for g in range(KVH):
        landed = pieces.at[pl.ds(g * per, per)]
        pltpu.make_async_copy(landed, landed, piece_sem.at[g]).wait()
        tall = jnp.concatenate(
            [pieces[g * per + j].astype(jnp.float32) for j in range(per)], axis=0
        )
        flat = jnp.transpose(tall).astype(jnp.bfloat16)
        for i in range(group):
            h = g * group + i
            out_ref[:, h * HD : (h + 1) * HD] = flat[i * rows : (i + 1) * rows]

    others = pl.ds(0, n - 1)
    for i, ref in ((0, q_all), (3, got_out), (4, got_ml), (5, pieces)):
        pltpu.make_async_copy(ref.at[others], ref.at[others], send_sem.at[i]).wait()

    @pl.when(me != 0)
    def _():
        pltpu.make_async_copy(k_own, k_own, send_sem.at[1]).wait()
        pltpu.make_async_copy(v_own, v_own, send_sem.at[2]).wait()


def solution(mesh):
    n = mesh.shape["seq"]

    def per_device(q, k, v, positions, span_segments, cache_keys, cache_values, cache_segments):
        rows, width = q.shape
        kwidth = k.shape[1]
        tokens = cache_keys.shape[0]
        share = KVH * HD // n
        bf16, f32, i32 = jnp.bfloat16, jnp.float32, jnp.int32
        return pl.pallas_call(
            functools.partial(kernel, n),
            out_shape=jax.ShapeDtypeStruct((rows, H * HD), bf16),
            in_specs=[pl.BlockSpec(memory_space=pl.ANY)] * 8,
            out_specs=pl.BlockSpec(memory_space=pltpu.VMEM),
            scratch_shapes=[
                pltpu.VMEM((rows, width), bf16),
                pltpu.VMEM((rows, kwidth), bf16),
                pltpu.VMEM((rows, kwidth), bf16),
                pltpu.SMEM(positions.shape, i32),
                pltpu.SMEM(span_segments.shape, i32),
                pltpu.VMEM((tokens, KVH * HD), bf16),
                pltpu.VMEM((tokens, KVH * HD), bf16),
                pltpu.VMEM((1, tokens), i32),
                pltpu.VMEM((n, rows, width), bf16),
                pltpu.VMEM((n, rows, kwidth), bf16),
                pltpu.VMEM((n, rows, kwidth), bf16),
                pltpu.VMEM((rows, KVH * HD), bf16),
                pltpu.VMEM((rows, KVH * HD), bf16),
                pltpu.VMEM((KVH, HD, tokens), bf16),
                pltpu.VMEM((tokens, HD), f32),
                pltpu.VMEM((n, share, HD), bf16),
                pltpu.VMEM((KVH, 2, HD), f32),
                pltpu.VMEM((n, share, HD), bf16),
                pltpu.VMEM((n, 2, HD), f32),
                pltpu.VMEM((share, HD), bf16),
                pltpu.VMEM((n, share, HD), bf16),
                pltpu.SemaphoreType.DMA((8,)),
                pltpu.SemaphoreType.DMA((KVH,)),
                pltpu.SemaphoreType.DMA((2,)),
                pltpu.SemaphoreType.DMA,
                pltpu.SemaphoreType.DMA,
                pltpu.SemaphoreType.DMA((KVH,)),
                pltpu.SemaphoreType.DMA((6,)),
            ],
            compiler_params=pltpu.CompilerParams(collective_id=0, has_side_effects=True),
        )(
            q,
            k,
            v,
            positions,
            span_segments,
            cache_keys,
            cache_values,
            cache_segments.reshape(1, tokens),
        )

    in_specs = (
        P(None, "seq"),
        P(None, "seq"),
        P(None, "seq"),
        P(),
        P(),
        P("seq", None),
        P("seq", None),
        P("seq"),
    )
    return jax.shard_map(
        per_device, mesh=mesh, in_specs=in_specs, out_specs=P(), check_vma=False
    )
```

time: 286 us -> 32.5 us (0.11)
  blocking collectives: 233 us -> 0 us
  Pallas kernels: 0 us -> 30.6 us
  waiting for transfers between devices: 14.7 us -> 0 us
  between operations: 14.1 us -> 0.01 us
  local copies, waits for them, and re-layouts: 14.1 us -> 1.67 us
  matrix products: 6.45 us -> 0 us
  other arithmetic: 3.34 us -> 0 us
    all_gather x4 -> x0, blocking collectives: 159 us -> none  [the longest x1 44.2 us: per_device(): lax.all_gather(queries, 'seq', axis=1, tiled=True)]
    unnamed x1 -> x0, blocking collectives: 36.9 us -> none
    pmax x1 -> x0, blocking collectives: 36.9 us -> none  [per_device(): peak = lax.pmax(local_peak, 'seq')]
    pallas_call x0 -> x1, Pallas kernels: none -> 30.6 us  [per_device(): pl.pallas_call(functools.partial(kernel, n), out_shape=jax.ShapeDtypeStru...]
    reduce_scatter x1 -> x0, waiting for transfers between devices: 14.6 us -> none  [per_device(): lax.psum_scatter(local_out * factor[:, None], 'seq', scatter_dimension=0,...]
    unnamed x92 -> x1, local copies, waits for them, and re-layouts: 8.67 us -> 1.67 us
    dot_general x32 -> x0, matrix products: 6.45 us -> none  [the longest x16 3.58 us: head_state(): lax.dot_general(block, key_cols, (((1,), (1,)), ((), ())), preferred_elem...]
    another operation x42 -> x0, local copies, waits for them, and re-layouts: 2.94 us -> none  [the longest x20 1.42 us: head_state(): total_all = jnp.stack(totals, axis=1).reshape(rows * kv_heads * group)]
  transfers between devices with their start and end apart: 1 -> 0, of which waited for: 1 -> 0; matrix products, arithmetic and copies ran while one was open for 2% -> 0% of each run, Pallas kernels for 0% -> 0%
where the time goes in v1:
time: 32.5 us; the launch traced here: 32.3 us
  Pallas kernels  30.6 us (94%)
  local copies, waits for them, and re-layouts  1.67 us (5%)
    pallas_call x1, Pallas kernels, per_device(): pl.pallas_call(functools.partial(kernel, n), out_shape=jax.ShapeDtypeStru...  30.6 us
    unnamed x1, local copies, waits for them, and re-layouts  1.67 us

profile of v1, /device:TPU:0, one launch (start us, length us, event | category | flops | bytes accessed | tf_op | source)
XLA Modules:
  0.0 32.3 jit_solution(10564743061596318588)
XLA Ops:
  0.0 30.6 %shard_map.82 = bf16[16,8192]{1,0:T(8,128)(2,1)} custom-call(bf16[16,256]{1,0:T(8,128)(2,1)} %q_hbm.1, bf16[16,32]{1,0:T(8,128)(2,1)} %k_hbm.1, bf16[16,32]{1,0:T(8,128)(2,1)} %v_hbm.1, s32[3,16]{1,0:T(4,128)} %pos_hbm.1, s32[16]{0:T(128)} %seg_hbm.1, bf16[512,1024]{1,0:T(8,128)(2,1)} %ck_hbm.1, bf16[512,1024]{1,0:T(8,128)(2,1)} %cv_hbm.1, s32[1,512]{1,0:T(1,128)} %bitcast.1), custom_call_target="tpu_custom_call" | custom-call | tf_op jit(solution)/shard_map/pallas_call | solution.py:325
  30.6 1.7 %copy.10 = bf16[16,8192]{1,0:T(8,128)(2,1)} copy(bf16[16,8192]{1,0:T(8,128)(2,1)} %shard_map.82) | data formatting | bytes 524288

commit v2 on v1

--- a/solution.py
+++ b/solution.py
@@ -46,6 +46,22 @@
     first = start // width
     return jnp.concatenate(
         [buf[first + i].astype(jnp.float32) for i in range(HD // width)], axis=1
+    )
+
+
+def group_head(buf, g, head):
+    width = buf.shape[3]
+    base = g * (buf.shape[1] // KVH)
+    if width >= HD:
+        block, off = head * HD // width, head * HD % width
+        return buf[block % 2, base + block // 2, :, off : off + HD].astype(jnp.float32)
+    first = head * (HD // width)
+    return jnp.concatenate(
+        [
+            buf[block % 2, base + block // 2].astype(jnp.float32)
+            for block in range(first, first + HD // width)
+        ],
+        axis=1,
     )
 
 
@@ -83,10 +99,12 @@
     pieces,
     load_sem,
     q_sem,
+    q_pair_sem,
     kv_sem,
     part_sem,
     ml_sem,
     piece_sem,
+    piece_pair_sem,
     send_sem,
 ):
     me = lax.axis_index("seq")
@@ -96,6 +114,27 @@
     per = n // KVH
     share = HD // per
     mine = me // per
+    half = per // 2
+    core, chip = lax.rem(me, 2), me // 2
+    pair = me + 1 - 2 * core
+
+    def hand_on(buf, g, sem, pair_sem, sent):
+        landed = buf.at[core, pl.ds(g * half, half)]
+        pltpu.make_async_copy(landed, landed, sem.at[g]).wait()
+        pltpu.make_async_remote_copy(
+            src_ref=landed,
+            dst_ref=landed,
+            send_sem=sent,
+            recv_sem=pair_sem.at[g],
+            device_id=(pair,),
+            device_id_type=MESH,
+        ).start()
+
+    def await_pair(buf, g, pair_sem):
+        landed = buf.at[1 - core, pl.ds(g * half, half)]
+        pltpu.make_async_copy(landed, landed, pair_sem.at[g]).wait()
+
+    order = [lax.rem(mine + t, KVH) for t in range(KVH)]
 
     loads = [
         pltpu.make_async_copy(src, dst, load_sem.at[i])
@@ -125,20 +164,9 @@
 
     for load in loads[:3]:
         load.wait()
-    own_q = pltpu.make_async_copy(q_own, q_all.at[me], q_sem.at[mine])
+    own_q = pltpu.make_async_copy(q_own, q_all.at[core, chip], q_sem.at[mine])
     own_q.start()
     pl.semaphore_wait(barrier, n - 1)
-
-    @pl.loop(1, n)
-    def _(i):
-        pltpu.make_async_remote_copy(
-            src_ref=q_own,
-            dst_ref=q_all.at[me],
-            send_sem=send_sem.at[0],
-            recv_sem=q_sem.at[mine],
-            device_id=(lax.rem(me + i, n),),
-            device_id_type=MESH,
-        ).start()
 
     @pl.when(me != 0)
     def _():
@@ -156,6 +184,17 @@
     def _():
         for i, (src, dst) in enumerate(((k_own, k_all), (v_own, v_all))):
             pltpu.make_async_copy(src, dst.at[me], kv_sem.at[i]).start()
+
+    @pl.loop(1, n // 2)
+    def _(i):
+        pltpu.make_async_remote_copy(
+            src_ref=q_own,
+            dst_ref=q_all.at[core, chip],
+            send_sem=send_sem.at[0],
+            recv_sem=q_sem.at[mine],
+            device_id=(lax.rem(me + 2 * i, n),),
+            device_id_type=MESH,
+        ).start()
 
     for load in loads[3:]:
         load.wait()
@@ -199,13 +238,15 @@
     contract_first = (((0,), (0,)), ((), ()))
     factor = math.log2(math.e) / math.sqrt(HD)
     group = H // KVH
-    for g in range(KVH):
-        cols = slice(g * HD, (g + 1) * HD)
-        landed = q_all.at[pl.ds(g * per, per)]
-        pltpu.make_async_copy(landed, landed, q_sem.at[g]).wait()
+    hand_on(q_all, order[0], q_sem, q_pair_sem, send_sem.at[6])
+    for t, g in enumerate(order):
+        cols = pl.ds(pl.multiple_of(g * HD, HD), HD)
+        if t + 1 < KVH:
+            hand_on(q_all, order[t + 1], q_sem, q_pair_sem, send_sem.at[6])
+        await_pair(q_all, g, q_pair_sem)
         heads = []
         for i in range(group):
-            q = columns(q_all, (g * group + i) * HD, width)
+            q = group_head(q_all, g, i)
             heads.append((q * cosine + pltpu.roll(q, HD // 2, 1) * sine).astype(jnp.bfloat16))
         block = jnp.concatenate(heads, axis=0)
         scores = (
@@ -235,8 +276,7 @@
             contract_first,
             preferred_element_type=jnp.float32,
         )
-        part_ml[g, 0:1, :] = peak
-        part_ml[g, 1:2, :] = total
+        part_ml[g] = jnp.concatenate([peak, total], axis=0)
         for j in range(per):
             part_out[g * per + j] = out[j * share : (j + 1) * share].astype(jnp.bfloat16)
 
@@ -279,33 +319,42 @@
         merged = merged + got_out[s].astype(jnp.float32) * scale[s : s + 1, :]
     piece[...] = merged.astype(jnp.bfloat16)
 
-    @pl.loop(1, n)
+    @pl.loop(1, n // 2)
     def _(i):
         pltpu.make_async_remote_copy(
             src_ref=piece,
-            dst_ref=pieces.at[me],
+            dst_ref=pieces.at[core, chip],
             send_sem=send_sem.at[5],
             recv_sem=piece_sem.at[mine],
-            device_id=(lax.rem(me + i, n),),
+            device_id=(lax.rem(me + 2 * i, n),),
             device_id_type=MESH,
         ).start()
 
-    pltpu.make_async_copy(piece, pieces.at[me], piece_sem.at[mine]).start()
-
-    for g in range(KVH):
-        landed = pieces.at[pl.ds(g * per, per)]
-        pltpu.make_async_copy(landed, landed, piece_sem.at[g]).wait()
+    pltpu.make_async_copy(piece, pieces.at[core, chip], piece_sem.at[mine]).start()
+
+    hand_on(pieces, order[0], piece_sem, piece_pair_sem, send_sem.at[7])
+    for t, g in enumerate(order):
+        if t + 1 < KVH:
+            hand_on(pieces, order[t + 1], piece_sem, piece_pair_sem, send_sem.at[7])
+        await_pair(pieces, g, piece_pair_sem)
         tall = jnp.concatenate(
-            [pieces[g * per + j].astype(jnp.float32) for j in range(per)], axis=0
+            [pieces[j % 2, g * half + j // 2].astype(jnp.float32) for j in range(per)], axis=0
         )
         flat = jnp.transpose(tall).astype(jnp.bfloat16)
         for i in range(group):
-            h = g * group + i
-            out_ref[:, h * HD : (h + 1) * HD] = flat[i * rows : (i + 1) * rows]
-
-    others = pl.ds(0, n - 1)
-    for i, ref in ((0, q_all), (3, got_out), (4, got_ml), (5, pieces)):
-        pltpu.make_async_copy(ref.at[others], ref.at[others], send_sem.at[i]).wait()
+            start = pl.multiple_of((g * group + i) * HD, HD)
+            out_ref[:, pl.ds(start, HD)] = flat[i * rows : (i + 1) * rows]
+
+    others, chips = pl.ds(0, n - 1), pl.ds(0, n // 2 - 1)
+    for i, ref in (
+        (0, q_all.at[0, chips]),
+        (3, got_out.at[others]),
+        (4, got_ml.at[others]),
+        (5, pieces.at[0, chips]),
+        (6, q_all.at[0]),
+        (7, pieces.at[0]),
+    ):
+        pltpu.make_async_copy(ref, ref, send_sem.at[i]).wait()
 
     @pl.when(me != 0)
     def _():
@@ -336,7 +385,7 @@
                 pltpu.VMEM((tokens, KVH * HD), bf16),
                 pltpu.VMEM((tokens, KVH * HD), bf16),
                 pltpu.VMEM((1, tokens), i32),
-                pltpu.VMEM((n, rows, width), bf16),
+                pltpu.VMEM((2, n // 2, rows, width), bf16),
                 pltpu.VMEM((n, rows, kwidth), bf16),
                 pltpu.VMEM((n, rows, kwidth), bf16),
                 pltpu.VMEM((rows, KVH * HD), bf16),
@@ -348,14 +397,16 @@
                 pltpu.VMEM((n, share, HD), bf16),
                 pltpu.VMEM((n, 2, HD), f32),
                 pltpu.VMEM((share, HD), bf16),
-                pltpu.VMEM((n, share, HD), bf16),
+                pltpu.VMEM((2, n // 2, share, HD), bf16),
                 pltpu.SemaphoreType.DMA((8,)),
+                pltpu.SemaphoreType.DMA((KVH,)),
                 pltpu.SemaphoreType.DMA((KVH,)),
                 pltpu.SemaphoreType.DMA((2,)),
                 pltpu.SemaphoreType.DMA,
                 pltpu.SemaphoreType.DMA,
                 pltpu.SemaphoreType.DMA((KVH,)),
-                pltpu.SemaphoreType.DMA((6,)),
+                pltpu.SemaphoreType.DMA((KVH,)),
+                pltpu.SemaphoreType.DMA((8,)),
             ],
             compiler_params=pltpu.CompilerParams(collective_id=0, has_side_effects=True),
         )(

time: 32.5 us -> 32.4 us (level)
  no operation moved by 1% of the time
where the time goes in v2:
time: 32.4 us; the launch traced here: 32.2 us
  Pallas kernels  30.5 us (94%)
  local copies, waits for them, and re-layouts  1.67 us (5%)
    pallas_call x1, Pallas kernels, per_device(): pl.pallas_call(functools.partial(kernel, n), out_shape=jax.ShapeDtypeStru...  30.5 us
    unnamed x1, local copies, waits for them, and re-layouts  1.67 us

profile of v2, /device:TPU:0, one launch (start us, length us, event | category | flops | bytes accessed | tf_op | source)
XLA Modules:
  0.0 32.2 jit_solution(4159295602225177642)
XLA Ops:
  0.0 30.5 %shard_map.82 = bf16[16,8192]{1,0:T(8,128)(2,1)} custom-call(bf16[16,256]{1,0:T(8,128)(2,1)} %q_hbm.1, bf16[16,32]{1,0:T(8,128)(2,1)} %k_hbm.1, bf16[16,32]{1,0:T(8,128)(2,1)} %v_hbm.1, s32[3,16]{1,0:T(4,128)} %pos_hbm.1, s32[16]{0:T(128)} %seg_hbm.1, bf16[512,1024]{1,0:T(8,128)(2,1)} %ck_hbm.1, bf16[512,1024]{1,0:T(8,128)(2,1)} %cv_hbm.1, s32[1,512]{1,0:T(1,128)} %bitcast.1), custom_call_target="tpu_custom_call" | custom-call | tf_op jit(solution)/shard_map/pallas_call | solution.py:374
  30.5 1.7 %copy.10 = bf16[16,8192]{1,0:T(8,128)(2,1)} copy(bf16[16,8192]{1,0:T(8,128)(2,1)} %shard_map.82) | data formatting | bytes 524288

commit v3 on v2

--- a/solution.py
+++ b/solution.py
@@ -99,12 +99,10 @@
     pieces,
     load_sem,
     q_sem,
-    q_pair_sem,
     kv_sem,
     part_sem,
     ml_sem,
     piece_sem,
-    piece_pair_sem,
     send_sem,
 ):
     me = lax.axis_index("seq")
@@ -116,23 +114,10 @@
     mine = me // per
     half = per // 2
     core, chip = lax.rem(me, 2), me // 2
-    pair = me + 1 - 2 * core
-
-    def hand_on(buf, g, sem, pair_sem, sent):
-        landed = buf.at[core, pl.ds(g * half, half)]
+
+    def await_group(buf, g, sem):
+        landed = buf.at[:, pl.ds(g * half, half)]
         pltpu.make_async_copy(landed, landed, sem.at[g]).wait()
-        pltpu.make_async_remote_copy(
-            src_ref=landed,
-            dst_ref=landed,
-            send_sem=sent,
-            recv_sem=pair_sem.at[g],
-            device_id=(pair,),
-            device_id_type=MESH,
-        ).start()
-
-    def await_pair(buf, g, pair_sem):
-        landed = buf.at[1 - core, pl.ds(g * half, half)]
-        pltpu.make_async_copy(landed, landed, pair_sem.at[g]).wait()
 
     order = [lax.rem(mine + t, KVH) for t in range(KVH)]
 
@@ -185,14 +170,14 @@
         for i, (src, dst) in enumerate(((k_own, k_all), (v_own, v_all))):
             pltpu.make_async_copy(src, dst.at[me], kv_sem.at[i]).start()
 
-    @pl.loop(1, n // 2)
+    @pl.loop(1, n)
     def _(i):
         pltpu.make_async_remote_copy(
             src_ref=q_own,
             dst_ref=q_all.at[core, chip],
             send_sem=send_sem.at[0],
             recv_sem=q_sem.at[mine],
-            device_id=(lax.rem(me + 2 * i, n),),
+            device_id=(lax.rem(me + i, n),),
             device_id_type=MESH,
         ).start()
 
@@ -238,12 +223,9 @@
     contract_first = (((0,), (0,)), ((), ()))
     factor = math.log2(math.e) / math.sqrt(HD)
     group = H // KVH
-    hand_on(q_all, order[0], q_sem, q_pair_sem, send_sem.at[6])
-    for t, g in enumerate(order):
+    for g in order:
         cols = pl.ds(pl.multiple_of(g * HD, HD), HD)
-        if t + 1 < KVH:
-            hand_on(q_all, order[t + 1], q_sem, q_pair_sem, send_sem.at[6])
-        await_pair(q_all, g, q_pair_sem)
+        await_group(q_all, g, q_sem)
         heads = []
         for i in range(group):
             q = group_head(q_all, g, i)
@@ -319,24 +301,21 @@
         merged = merged + got_out[s].astype(jnp.float32) * scale[s : s + 1, :]
     piece[...] = merged.astype(jnp.bfloat16)
 
-    @pl.loop(1, n // 2)
+    @pl.loop(1, n)
     def _(i):
         pltpu.make_async_remote_copy(
             src_ref=piece,
             dst_ref=pieces.at[core, chip],
             send_sem=send_sem.at[5],
             recv_sem=piece_sem.at[mine],
-            device_id=(lax.rem(me + 2 * i, n),),
+            device_id=(lax.rem(me + i, n),),
             device_id_type=MESH,
         ).start()
 
     pltpu.make_async_copy(piece, pieces.at[core, chip], piece_sem.at[mine]).start()
 
-    hand_on(pieces, order[0], piece_sem, piece_pair_sem, send_sem.at[7])
-    for t, g in enumerate(order):
-        if t + 1 < KVH:
-            hand_on(pieces, order[t + 1], piece_sem, piece_pair_sem, send_sem.at[7])
-        await_pair(pieces, g, piece_pair_sem)
+    for g in order:
+        await_group(pieces, g, piece_sem)
         tall = jnp.concatenate(
             [pieces[j % 2, g * half + j // 2].astype(jnp.float32) for j in range(per)], axis=0
         )
@@ -351,8 +330,8 @@
         (3, got_out.at[others]),
         (4, got_ml.at[others]),
         (5, pieces.at[0, chips]),
-        (6, q_all.at[0]),
-        (7, pieces.at[0]),
+        (0, q_all.at[1]),
+        (5, pieces.at[1]),
     ):
         pltpu.make_async_copy(ref, ref, send_sem.at[i]).wait()
 
@@ -400,13 +379,11 @@
                 pltpu.VMEM((2, n // 2, share, HD), bf16),
                 pltpu.SemaphoreType.DMA((8,)),
                 pltpu.SemaphoreType.DMA((KVH,)),
-                pltpu.SemaphoreType.DMA((KVH,)),
                 pltpu.SemaphoreType.DMA((2,)),
                 pltpu.SemaphoreType.DMA,
                 pltpu.SemaphoreType.DMA,
                 pltpu.SemaphoreType.DMA((KVH,)),
-                pltpu.SemaphoreType.DMA((KVH,)),
-                pltpu.SemaphoreType.DMA((8,)),
+                pltpu.SemaphoreType.DMA((6,)),
             ],
             compiler_params=pltpu.CompilerParams(collective_id=0, has_side_effects=True),
         )(

time: 32.4 us -> 32.2 us (level)
  no operation moved by 1% of the time
where the time goes in v3:
time: 32.2 us; the launch traced here: 32 us
  Pallas kernels  30.3 us (94%)
  local copies, waits for them, and re-layouts  1.67 us (5%)
    pallas_call x1, Pallas kernels, per_device(): pl.pallas_call(functools.partial(kernel, n), out_shape=jax.ShapeDtypeStru...  30.3 us
    unnamed x1, local copies, waits for them, and re-layouts  1.67 us

profile of v3, /device:TPU:0, one launch (start us, length us, event | category | flops | bytes accessed | tf_op | source)
XLA Modules:
  0.0 32.0 jit_solution(3971594874184605179)
XLA Ops:
  0.0 30.3 %shard_map.82 = bf16[16,8192]{1,0:T(8,128)(2,1)} custom-call(bf16[16,256]{1,0:T(8,128)(2,1)} %q_hbm.1, bf16[16,32]{1,0:T(8,128)(2,1)} %k_hbm.1, bf16[16,32]{1,0:T(8,128)(2,1)} %v_hbm.1, s32[3,16]{1,0:T(4,128)} %pos_hbm.1, s32[16]{0:T(128)} %seg_hbm.1, bf16[512,1024]{1,0:T(8,128)(2,1)} %ck_hbm.1, bf16[512,1024]{1,0:T(8,128)(2,1)} %cv_hbm.1, s32[1,512]{1,0:T(1,128)} %bitcast.1), custom_call_target="tpu_custom_call" | custom-call | tf_op jit(solution)/shard_map/pallas_call | solution.py:353
  30.3 1.7 %copy.10 = bf16[16,8192]{1,0:T(8,128)(2,1)} copy(bf16[16,8192]{1,0:T(8,128)(2,1)} %shard_map.82) | data formatting | bytes 524288
